TPU v7x, 32 devices: a whole 2x2x4 slice. The times are simulated.
32 devices in a mesh: srv: 16 (over z, y, x), grp: 2 (over core).
Axes of the slice: x: 2, y: 2, z: 4, core: 2. Of those that a mesh axis runs over, the one named last changes fastest.
Arguments:
- basis_modes: float32 [64, 64, 3072], P(None, ('srv', 'grp')), may hold values from -10 to 10
- weights: float32 [64], replicated, may hold values from 0.5 to 4
- snapshots: float32 [16, 64, 3072], P(None, 'srv', 'grp'), may hold values from -10 to 10
Outputs:
- new_modes: float32 [80, 64, 3072], P(None, ('srv', 'grp'))
- factor: float32 [80, 80], replicated
All inputs are finite; a program needn't handle non-finite values.
Results may differ from a plain program's by a relative error of at most 0.00009.
Values sent between devices are 32-bit elements; how exact they have to be, the bound alone decides.
No kernel may reach another device: no remote copies, remote signals or barrier semaphores. Data moves between devices by JAX's collectives and lax.ppermute only.
A program may use at most 64 MiB of HBM per device.

v0:
```python
import jax
import jax.numpy as jnp
from jax import lax
from jax.sharding import PartitionSpec as P

MODES = 64
SNAPS = 16


def merged_factor(local_gram):
    return jnp.linalg.cholesky(lax.psum(local_gram, ("srv", "grp")))


def per_device(basis_modes, weights, snapshots):
    width = MODES + SNAPS
    total_cells = (
        basis_modes.shape[1] * basis_modes.shape[2] * lax.axis_size("srv") * lax.axis_size("grp")
    )
    scaled = basis_modes * weights[:, None, None]
    arrived = lax.all_to_all(snapshots, "grp", split_axis=1, concat_axis=2, tiled=True)
    panel = jnp.concatenate([scaled, arrived], axis=0).reshape(width, -1)
    local_gram = (
        jnp.dot(panel, panel.T, precision=lax.Precision.HIGHEST, preferred_element_type=jnp.float32)
        / total_cells
    )
    factor = merged_factor(local_gram)
    inverse = lax.linalg.triangular_solve(
        factor, jnp.eye(width, dtype=jnp.float32), left_side=True, lower=True
    )
    result = jnp.dot(
        inverse, panel, precision=lax.Precision.HIGHEST, preferred_element_type=jnp.float32
    )
    result = result.reshape(width, basis_modes.shape[1], basis_modes.shape[2])
    return (result, factor)


def solution(mesh):
    in_specs = (P(None, ("srv", "grp"), None), P(), P(None, "srv", "grp"))
    out_specs = (P(None, ("srv", "grp"), None), P())
    return jax.shard_map(
        per_device, mesh=mesh, in_specs=in_specs, out_specs=out_specs, check_vma=False
    )
```

profile of v0, /device:TPU:0, one launch (start us, length us, event | category | flops | bytes accessed | tf_op | source)
XLA Modules:
  0.0 77.2 jit_solution(11390154502908591722)
XLA Ops:
  0.6 0.0 copy-start
  0.6 0.0 copy-start.1
  0.6 1.2 %copy.19 = f32[16,4,1536]{2,0,1:T(8,128)S(1)} copy(f32[16,4,1536]{2,1,0:T(4,128)} %param.5) | data formatting | bytes 786432 | tf_op args[2]
  1.9 4.0 %all_to_all.18 = f32[16,4,1536]{2,0,1:T(8,128)S(1)} all-to-all(f32[16,4,1536]{2,0,1:T(8,128)S(1)} %copy.19), channel_id=1, replica_groups=mesh['srv'=16,'grp'=2] {'grp'}, dimensions={1} | all-to-all | bytes 786432 | tf_op jit(solution)/shard_map/all_to_all | solution.py:20
  5.9 1.1 %copy.41 = f32[16,2,2,1536]{3,1,0,2:T(2,128)} copy(f32[16,2,2,1536]{3,0,2,1:T(8,128)S(1)} %bitcast.35) | data formatting | bytes 786432 | tf_op jit(solution)/shard_map/all_to_all | solution.py:20
  7.0 0.3 copy.42
  7.3 0.0 copy-done
  7.3 0.0 copy-done.1
  7.3 0.5 copy_multiply_fusion
  7.8 0.5 fusion.17
  8.4 2.1 %all_to_all.16 = f32[16,2,3072]{2,0,1:T(8,128)} reshape(f32[16,2,2,1536]{3,2,0,1:T(2,128)} %bitcast.38) | data formatting | bytes 786432 | tf_op jit(solution)/shard_map/all_to_all | solution.py:20
  10.4 3.4 %fusion.10 = f32[80,80]{0,1:T(8,128)} fusion(f32[16,2,3072]{2,0,1:T(8,128)} %all_to_all.16, f32[64,2,3072]{2,0,1:T(8,128)S(1)} %copy_multiply_fusion), kind=kOutput, calls=%fused_computation.11 | convolution fusion | flops 472357120 | bytes 1991680 | tf_op jit(solution)/shard_map/dot_general | solution.py:23
  13.9 42.4 %psum.7 = f32[80,80]{0,1:T(8,128)S(1)} all-reduce(f32[80,80]{0,1:T(8,128)} %fusion.10), channel_id=1, replica_groups=mesh['srv'=16,'grp'=2] {'srv','grp'}, use_global_device_ids=true, to_apply=%region_0.0 | all-reduce | flops 6400 | bytes 51200 | tf_op jit(solution)/shard_map/psum | solution.py:11
  56.2 0.1 copy.23
  56.3 7.3 %cholesky.17 = f32[80,80]{1,0:T(8,128)S(1)} custom-call(f32[80,80]{1,0:T(8,128)S(1)} %fusion.14), custom_call_target="Cholesky" | custom-call | tf_op jit(solution)/shard_map/jit(cholesky)/cholesky | solution.py:11
  63.7 0.6 compare_reduce_fusion
  64.3 1.3 %select_bitcast_fusion = (f32[1,80,80]{2,1,0:T(8,128)S(1)}, f32[80,80]{1,0:T(8,128)}) fusion(f32[80,80]{1,0:T(8,128)S(1)} %cholesky.17, pred[]{:T(512)} %compare_reduce_fusion), kind=kLoop, calls=%fused_computation.17 | loop fusion | flops 25600 | bytes 76801 | tf_op jit(solution)/shard_map/triangular_solve | solution.py:27
  65.6 6.1 %custom-call.6 = f32[1,80,80]{1,2,0:T(8,128)S(1)} custom-call(f32[1,80,80]{2,1,0:T(8,128)S(1)} %get-tuple-element.8), custom_call_target="InvertDiagBlocksLowerTriangular" | custom-call | tf_op jit(solution)/shard_map/triangular_solve | solution.py:27
  71.7 0.2 convolution_bitcast_fusion
  72.0 0.3 concatenate.12
  72.3 0.1 copy.31
  72.4 0.1 pad_maximum_fusion
  72.6 1.8 %fusion = f32[80,2,3072]{2,0,1:T(8,128)S(1)} fusion(f32[80,80,1]{1,0,2:T(8,128)S(1)} %convolution_bitcast_fusion, f32[10,2,8,3072]{3,2,1,0:T(8,128)S(1)} %bitcast.33), kind=kOutput, calls=%fused_computation | convolution fusion | flops 471859200 | bytes 3957760 | tf_op jit(solution)/shard_map/dot_general | solution.py:30
  74.4 2.8 %copy.26 = f32[80,2,3072]{2,1,0:T(2,128)} copy(f32[80,2,3072]{2,0,1:T(8,128)S(1)} %fusion) | data formatting | bytes 3932160
  (2 shorter events, 0.0 us)
Async XLA Ops:
  0.6 6.7 %copy-start = (f32[64,2,3072]{2,1,0:T(2,128)S(1)}, f32[64,2,3072]{2,1,0:T(2,128)}, u32[]{:S(2)}) copy-start(f32[64,2,3072]{2,1,0:T(2,128)} %param.3) | copy-start | bytes 4718596
  0.6 6.7 %copy-start.1 = (f32[64]{0:T(128)S(1)}, f32[64]{0:T(128)}, u32[]{:S(2)}) copy-start(f32[64]{0:T(128)} %param.4) | copy-start | bytes 772
where the time goes:
time: 77.6 us; the launch traced here: 77.2 us
  blocking collectives  46.4 us (60%)
  other arithmetic  16.6 us (21%)
  local copies, waits for them, and re-layouts  7.98 us (10%)
  matrix products  5.45 us (7%)
    psum x1, blocking collectives, merged_factor(): return jnp.linalg.cholesky(lax.psum(local_gram, ('srv', 'grp')))  42.4 us
    another operation x3, other arithmetic, merged_factor(): return jnp.linalg.cholesky(lax.psum(local_gram, ('srv', 'grp')))  7.98 us
    another operation x2, other arithmetic, per_device(): lax.linalg.triangular_solve(factor, jnp.eye(width, dtype=jnp.float32), le...  7.4 us
    all_to_all x1, blocking collectives, per_device(): lax.all_to_all(snapshots, 'grp', split_axis=1, concat_axis=2, tiled=True)  4.05 us
    unnamed x6, local copies, waits for them, and re-layouts  4.04 us
    all_to_all x3, local copies, waits for them, and re-layouts, per_device(): lax.all_to_all(snapshots, 'grp', split_axis=1, concat_axis=2, tiled=True)  3.43 us
    dot_general x1, matrix products, per_device(): jnp.dot(panel, panel.T, precision=lax.Precision.HIGHEST, preferred_elemen...  3.41 us
    dot_general x1, matrix products, per_device(): jnp.dot(inverse, panel, precision=lax.Precision.HIGHEST, preferred_elemen...  1.82 us

commit v1 on v0

--- a/solution.py
+++ b/solution.py
@@ -8,7 +8,7 @@
 
 
 def merged_factor(local_gram):
-    return jnp.linalg.cholesky(lax.psum(local_gram, ("srv", "grp")))
+    return jnp.linalg.cholesky(jnp.sum(lax.all_gather(local_gram, ("srv", "grp")), axis=0))
 
 
 def per_device(basis_modes, weights, snapshots):

time: 77.6 us -> 81.6 us (1.052)
  blocking collectives: 46.4 us -> 51.1 us
    all_gather x0 -> x1, blocking collectives: none -> 47 us  [merged_factor(): lax.all_gather(local_gram, ('srv', 'grp'))]
    psum x1 -> x0, blocking collectives: 42.4 us -> none  [merged_factor(): return jnp.linalg.cholesky(lax.psum(local_gram, ('srv', 'grp')))]
where the time goes in v1:
time: 81.6 us; the launch traced here: 81.3 us
  blocking collectives  51.1 us (63%)
  other arithmetic  16.7 us (20%)
  local copies, waits for them, and re-layouts  7.99 us (10%)
  matrix products  4.83 us (6%)
    all_gather x1, blocking collectives, merged_factor(): lax.all_gather(local_gram, ('srv', 'grp'))  47 us
    another operation x3, other arithmetic, merged_factor(): jnp.linalg.cholesky(jnp.sum(lax.all_gather(local_gram, ('srv', 'grp')), a...  7.98 us
    another operation x2, other arithmetic, per_device(): lax.linalg.triangular_solve(factor, jnp.eye(width, dtype=jnp.float32), le...  7.4 us
    all_to_all x1, blocking collectives, per_device(): lax.all_to_all(snapshots, 'grp', split_axis=1, concat_axis=2, tiled=True)  4.05 us
    unnamed x6, local copies, waits for them, and re-layouts  4.04 us
    all_to_all x3, local copies, waits for them, and re-layouts, per_device(): lax.all_to_all(snapshots, 'grp', split_axis=1, concat_axis=2, tiled=True)  3.43 us
    dot_general x1, matrix products, per_device(): jnp.dot(panel, panel.T, precision=lax.Precision.HIGHEST, preferred_elemen...  2.79 us
    dot_general x1, matrix products, per_device(): jnp.dot(inverse, panel, precision=lax.Precision.HIGHEST, preferred_elemen...  1.82 us

profile of v1, /device:TPU:0, one launch (start us, length us, event | category | flops | bytes accessed | tf_op | source)
XLA Modules:
  0.0 81.3 jit_solution(8295753857637908935)
XLA Ops:
  0.6 0.0 copy-start
  0.6 0.0 copy-start.1
  0.6 1.2 %copy.17 = f32[16,4,1536]{2,0,1:T(8,128)S(1)} copy(f32[16,4,1536]{2,1,0:T(4,128)} %param.5) | data formatting | bytes 786432 | tf_op args[2]
  1.9 4.0 %all_to_all.18 = f32[16,4,1536]{2,0,1:T(8,128)S(1)} all-to-all(f32[16,4,1536]{2,0,1:T(8,128)S(1)} %copy.17), channel_id=1, replica_groups=mesh['srv'=16,'grp'=2] {'grp'}, dimensions={1} | all-to-all | bytes 786432 | tf_op jit(solution)/shard_map/all_to_all | solution.py:20
  5.9 1.1 %copy.36 = f32[16,2,2,1536]{3,1,0,2:T(2,128)} copy(f32[16,2,2,1536]{3,0,2,1:T(8,128)S(1)} %bitcast.37) | data formatting | bytes 786432 | tf_op jit(solution)/shard_map/all_to_all | solution.py:20
  7.0 0.3 copy.37
  7.3 0.0 copy-done
  7.3 0.0 copy-done.1
  7.3 0.5 copy_multiply_fusion
  7.8 0.5 fusion.17
  8.4 2.1 %all_to_all.16 = f32[16,2,3072]{2,0,1:T(8,128)} reshape(f32[16,2,2,1536]{3,2,0,1:T(2,128)} %bitcast.40) | data formatting | bytes 786432 | tf_op jit(solution)/shard_map/all_to_all | solution.py:20
  10.4 2.8 %fusion.10 = f32[80,80]{1,0:T(8,128)S(1)} fusion(f32[16,2,3072]{2,0,1:T(8,128)} %all_to_all.16, f32[64,2,3072]{2,0,1:T(8,128)S(1)} %copy_multiply_fusion), kind=kOutput, calls=%fused_computation.11 | convolution fusion | flops 472357120 | bytes 1991680 | tf_op jit(solution)/shard_map/dot_general | solution.py:23
  13.2 47.0 %all-gather = f32[2560,80]{1,0:T(8,128)S(1)} all-gather(f32[80,80]{1,0:T(8,128)S(1)} %fusion.10), channel_id=2, replica_groups=mesh['srv'=16,'grp'=2] {'srv','grp'}, dimensions={0}, use_global_device_ids=true | all-gather | bytes 844800 | tf_op jit(solution)/shard_map/all_gather | solution.py:11
  60.3 0.1 reduce_sum.9
  60.4 0.1 copy.20
  60.5 7.3 %cholesky.17 = f32[80,80]{1,0:T(8,128)S(1)} custom-call(f32[80,80]{1,0:T(8,128)S(1)} %fusion.14), custom_call_target="Cholesky" | custom-call | tf_op jit(solution)/shard_map/jit(cholesky)/cholesky | solution.py:11
  67.8 0.6 compare_reduce_fusion
  68.5 1.3 %select_bitcast_fusion = (f32[1,80,80]{2,1,0:T(8,128)S(1)}, f32[80,80]{1,0:T(8,128)}) fusion(f32[80,80]{1,0:T(8,128)S(1)} %cholesky.17, pred[]{:T(512)} %compare_reduce_fusion), kind=kLoop, calls=%fused_computation.17 | loop fusion | flops 25600 | bytes 76801 | tf_op jit(solution)/shard_map/triangular_solve | solution.py:27
  69.7 6.1 %custom-call.6 = f32[1,80,80]{1,2,0:T(8,128)S(1)} custom-call(f32[1,80,80]{2,1,0:T(8,128)S(1)} %get-tuple-element.8), custom_call_target="InvertDiagBlocksLowerTriangular" | custom-call | tf_op jit(solution)/shard_map/triangular_solve | solution.py:27
  75.9 0.2 convolution_bitcast_fusion
  76.1 0.3 concatenate.12
  76.4 0.1 copy.26
  76.5 0.1 pad_maximum_fusion
  76.7 1.8 %fusion = f32[80,2,3072]{2,0,1:T(8,128)S(1)} fusion(f32[80,80,1]{1,0,2:T(8,128)S(1)} %convolution_bitcast_fusion, f32[10,2,8,3072]{3,2,1,0:T(8,128)S(1)} %bitcast.34), kind=kOutput, calls=%fused_computation | convolution fusion | flops 471859200 | bytes 3957760 | tf_op jit(solution)/shard_map/dot_general | solution.py:30
  78.5 2.8 %copy.23 = f32[80,2,3072]{2,1,0:T(2,128)} copy(f32[80,2,3072]{2,0,1:T(8,128)S(1)} %fusion) | data formatting | bytes 3932160
  (2 shorter events, 0.0 us)
Async XLA Ops:
  0.6 6.7 %copy-start = (f32[64,2,3072]{2,1,0:T(2,128)S(1)}, f32[64,2,3072]{2,1,0:T(2,128)}, u32[]{:S(2)}) copy-start(f32[64,2,3072]{2,1,0:T(2,128)} %param.3) | copy-start | bytes 4718596
  0.6 6.7 %copy-start.1 = (f32[64]{0:T(128)S(1)}, f32[64]{0:T(128)}, u32[]{:S(2)}) copy-start(f32[64]{0:T(128)} %param.4) | copy-start | bytes 772

commit v2 on v0

--- a/solution.py
+++ b/solution.py
@@ -8,7 +8,7 @@
 
 
 def merged_factor(local_gram):
-    return jnp.linalg.cholesky(lax.psum(local_gram, ("srv", "grp")))
+    return jnp.linalg.cholesky(lax.psum(lax.psum(local_gram, "srv"), "grp"))
 
 
 def per_device(basis_modes, weights, snapshots):

time: 77.6 us -> 118 us (1.52)
  blocking collectives: 46.4 us -> 86.8 us
    psum x1 -> x2, blocking collectives: 42.4 us -> 82.7 us  [merged_factor(): return jnp.linalg.cholesky(lax.psum(lax.psum(local_gram, 'srv'), 'grp'))]
where the time goes in v2:
time: 118 us
  blocking collectives  86.8 us (74%)
  other arithmetic  16.6 us (14%)
  local copies, waits for them, and re-layouts  7.98 us (7%)
  matrix products  5.45 us (5%)
    psum x2, blocking collectives, merged_factor(): return jnp.linalg.cholesky(lax.psum(lax.psum(local_gram, 'srv'), 'grp'))  82.7 us
    another operation x3, other arithmetic, merged_factor(): return jnp.linalg.cholesky(lax.psum(lax.psum(local_gram, 'srv'), 'grp'))  7.98 us
    another operation x2, other arithmetic, per_device(): lax.linalg.triangular_solve(factor, jnp.eye(width, dtype=jnp.float32), le...  7.4 us
    all_to_all x1, blocking collectives, per_device(): lax.all_to_all(snapshots, 'grp', split_axis=1, concat_axis=2, tiled=True)  4.05 us
    unnamed x6, local copies, waits for them, and re-layouts  4.04 us
    all_to_all x3, local copies, waits for them, and re-layouts, per_device(): lax.all_to_all(snapshots, 'grp', split_axis=1, concat_axis=2, tiled=True)  3.43 us
    dot_general x1, matrix products, per_device(): jnp.dot(panel, panel.T, precision=lax.Precision.HIGHEST, preferred_elemen...  3.41 us

profile of v2, /device:TPU:0, one launch (start us, length us, event | category | flops | bytes accessed | tf_op | source)
XLA Modules:
  0.0 117.5 jit_solution(6581803728543397810)
XLA Ops:
  0.6 0.0 copy-start
  0.6 0.0 copy-start.1
  0.6 1.2 %copy.19 = f32[16,4,1536]{2,0,1:T(8,128)S(1)} copy(f32[16,4,1536]{2,1,0:T(4,128)} %param.5) | data formatting | bytes 786432 | tf_op args[2]
  1.9 4.0 %all_to_all.18 = f32[16,4,1536]{2,0,1:T(8,128)S(1)} all-to-all(f32[16,4,1536]{2,0,1:T(8,128)S(1)} %copy.19), channel_id=1, replica_groups=mesh['srv'=16,'grp'=2] {'grp'}, dimensions={1} | all-to-all | bytes 786432 | tf_op jit(solution)/shard_map/all_to_all | solution.py:20
  5.9 1.1 copy.41
  7.0 0.3 copy.42
  7.3 0.0 copy-done
  7.3 0.0 copy-done.1
  7.3 0.5 copy_multiply_fusion
  7.8 0.5 fusion.17
  8.4 2.1 %all_to_all.16 = f32[16,2,3072]{2,0,1:T(8,128)} reshape(f32[16,2,2,1536]{3,2,0,1:T(2,128)} %bitcast.38) | data formatting | bytes 786432 | tf_op jit(solution)/shard_map/all_to_all | solution.py:20
  10.4 3.4 %fusion.10 = f32[80,80]{0,1:T(8,128)} fusion(f32[16,2,3072]{2,0,1:T(8,128)} %all_to_all.16, f32[64,2,3072]{2,0,1:T(8,128)S(1)} %copy_multiply_fusion), kind=kOutput, calls=%fused_computation.11 | convolution fusion | flops 472357120 | bytes 1991680 | tf_op jit(solution)/shard_map/dot_general | solution.py:23
  13.9 79.3 %psum.14 = f32[80,80]{0,1:T(8,128)S(1)} all-reduce(f32[80,80]{0,1:T(8,128)} %fusion.10), channel_id=1, replica_groups=mesh['srv'=16,'grp'=2] {'srv'}, use_global_device_ids=true, to_apply=%region_0.0 | all-reduce | flops 6400 | bytes 51200 | tf_op jit(solution)/shard_map/psum | solution.py:11
  93.1 3.5 %psum.15 = f32[80,80]{0,1:T(8,128)S(1)} all-reduce(f32[80,80]{0,1:T(8,128)S(1)} %psum.14), channel_id=1, replica_groups=mesh['srv'=16,'grp'=2] {'grp'}, use_global_device_ids=true, to_apply=%region_1.0 | all-reduce | flops 6400 | bytes 51200 | tf_op jit(solution)/shard_map/psum | solution.py:11
  96.6 0.1 copy.23
  96.7 7.3 %cholesky.17 = f32[80,80]{1,0:T(8,128)S(1)} custom-call(f32[80,80]{1,0:T(8,128)S(1)} %fusion.14), custom_call_target="Cholesky" | custom-call | tf_op jit(solution)/shard_map/jit(cholesky)/cholesky | solution.py:11
  104.0 0.6 compare_reduce_fusion
  104.7 1.3 %select_bitcast_fusion = (f32[1,80,80]{2,1,0:T(8,128)S(1)}, f32[80,80]{1,0:T(8,128)}) fusion(f32[80,80]{1,0:T(8,128)S(1)} %cholesky.17, pred[]{:T(512)} %compare_reduce_fusion), kind=kLoop, calls=%fused_computation.17 | loop fusion | flops 25600 | bytes 76801 | tf_op jit(solution)/shard_map/triangular_solve | solution.py:27
  105.9 6.1 %custom-call.6 = f32[1,80,80]{1,2,0:T(8,128)S(1)} custom-call(f32[1,80,80]{2,1,0:T(8,128)S(1)} %get-tuple-element.8), custom_call_target="InvertDiagBlocksLowerTriangular" | custom-call | tf_op jit(solution)/shard_map/triangular_solve | solution.py:27
  112.1 0.2 convolution_bitcast_fusion
  112.3 0.3 concatenate.12
  112.7 0.1 copy.31
  112.8 0.1 pad_maximum_fusion
  112.9 1.8 %fusion = f32[80,2,3072]{2,0,1:T(8,128)S(1)} fusion(f32[80,80,1]{1,0,2:T(8,128)S(1)} %convolution_bitcast_fusion, f32[10,2,8,3072]{3,2,1,0:T(8,128)S(1)} %bitcast.33), kind=kOutput, calls=%fused_computation | convolution fusion | flops 471859200 | bytes 3957760 | tf_op jit(solution)/shard_map/dot_general | solution.py:30
  114.7 2.8 %copy.26 = f32[80,2,3072]{2,1,0:T(2,128)} copy(f32[80,2,3072]{2,0,1:T(8,128)S(1)} %fusion) | data formatting | bytes 3932160
  (2 shorter events, 0.0 us)
Async XLA Ops:
  0.6 6.7 %copy-start = (f32[64,2,3072]{2,1,0:T(2,128)S(1)}, f32[64,2,3072]{2,1,0:T(2,128)}, u32[]{:S(2)}) copy-start(f32[64,2,3072]{2,1,0:T(2,128)} %param.3) | copy-start | bytes 4718596
  0.6 6.7 %copy-start.1 = (f32[64]{0:T(128)S(1)}, f32[64]{0:T(128)}, u32[]{:S(2)}) copy-start(f32[64]{0:T(128)} %param.4) | copy-start | bytes 772
